TPU v7x, 256 devices: a 2x2x32 block of a 4x8x32 slice. The times are simulated.
256 devices in a mesh: grp: 4 (over x, y), space: 64 (over z, core).
Axes of the slice: x: 2, y: 2, z: 32, core: 2. Of those that a mesh axis runs over, the one named last changes fastest.
The devices are a block of a 4x8x32 slice.
Arguments:
- propagator: bfloat16 [8, 3, 4, 12, 131072], P('grp', None, None, None, 'space'), parts along dimension 0, may hold values from -6 to 6
- eigvecs: bfloat16 [8, 3, 256, 131072], P('grp', None, None, 'space'), parts along dimension 0, may hold values from -16 to 16
- operator_weights: float32 [512, 2, 256], P('grp'), parts along dimension 0, may hold values from -0.375 to 0.375
- sink_time: int32 [4], P('grp'), parts along dimension 0, may hold values from 0 to 127
- term_index: int32 [48, 3], replicated, may hold values from 0 to 11
- term_sign: int32 [48], replicated, may hold values from 0 to 1
- solver_order: int32 [131072], P('space'), may hold values from 0 to 131071, as said below
Outputs:
- solver_source: bfloat16 [8, 3, 4, 12, 131072], P('grp', None, None, None, 'space'), parts along dimension 0
There are 4 independent parts, one for each index of `grp`. A program takes and returns all parts, laid end to end along the dimension named above; an argument that names none is the same for every part. Nothing has to cross between parts.
Inputs may be any that keep to these rules, and one draw needn't show every extreme that they name: solver_order is a permutation of the sites; split into blocks of 2048 positions and each block into pieces of 32, piece d of block e holds only sites d * 2048 to (d + 1) * 2048 - 1.
All inputs are finite; a program needn't handle non-finite values.
Results may differ from a plain program's by a relative error of at most 0.006.
Values may be sent and summed in bfloat16 or wider, within the bound.
A program may use at most 64 MiB of HBM per device.

v0:
```python
import math

import jax
import jax.numpy as jnp
from jax import lax
from jax.sharding import Mesh
from jax.sharding import PartitionSpec as P

NVEC = 256
NMOM = 4
EXTENT = 64
SPACE = ("space_0", "space_1")


MOMENTA = ((0, 0, 0), (1, 0, 0), (0, 1, 0), (0, 0, 1))
PRECISE = lax.Precision.HIGHEST


def rows_for(lines, count):
    spare = -lines.shape[0] % count
    if not spare:
        return lines
    return jnp.concatenate([lines, jnp.zeros((spare, *lines.shape[1:]), lines.dtype)])


def own_block(blocks, axes, sequence):
    inside = blocks.shape[1:]
    blocks = blocks.reshape(*(lax.axis_size(a) for a in axes), *inside)
    blocks = jnp.moveaxis(blocks, sequence, range(len(axes))).reshape(-1, *inside)
    for k in sequence:
        blocks = lax.psum_scatter(blocks, axes[k], scatter_dimension=0, tiled=True)
    return blocks[0]


def all_blocks(x, axes, sequence):
    blocks = x
    for k in sequence:
        blocks = lax.all_gather(blocks, axes[k])
    done = sequence[::-1]
    back = [done.index(k) for k in range(len(axes))]
    blocks = blocks.transpose(*back, *range(len(axes), blocks.ndim))
    return blocks.reshape(-1, *x.shape)


def sum_all_axes(x, axes):
    size, count = (lax.axis_size(axes), len(axes))
    lines = x.reshape(-1, *x.shape[1:][-1:])
    blocks = rows_for(lines, size * count).reshape(count, size, -1, *lines.shape[1:])
    outs = []
    for initial in range(count):
        sequence = [(initial + k) % count for k in range(count)]
        own = own_block(blocks[initial], axes, sequence)
        outs.append(all_blocks(own, axes, sequence[::-1]).reshape(-1, *lines.shape[1:]))
    return jnp.concatenate(outs)[: len(lines)].reshape(x.shape)


def in_blocks(x, dim, count):
    before, after = (x.shape[:dim], x.shape[dim + 1 :])
    return jnp.moveaxis(x.reshape(*before, count, -1, *after), dim, 0)


def joined_along(blocks, dim):
    lengths = list(blocks.shape[1:])
    lengths[dim] *= blocks.shape[0]
    return jnp.moveaxis(blocks, 0, dim).reshape(lengths)


def exchange_in_order(blocks, axes, sequence):
    lengths = [lax.axis_size(a) for a in axes]
    blocks = blocks.reshape(*lengths, *blocks.shape[1:])
    for k in sequence:
        blocks = lax.all_to_all(blocks, axes[k], split_axis=k, concat_axis=k, tiled=True)
    return blocks.reshape(-1, *blocks.shape[len(axes) :])


def core_and_chips(x, groups, sequence, split_dim, concat_dim):
    count = lax.axis_size(groups[0]) * lax.axis_size(groups[1])
    blocks = in_blocks(x, split_dim, count)
    return joined_along(exchange_in_order(blocks, groups, sequence), concat_dim)


def phase_tables(offset, length):
    site_index = offset + jnp.arange(length, dtype=jnp.int32)
    coord_x = site_index % EXTENT
    coord_y = site_index // EXTENT % EXTENT
    coord_z = site_index // (EXTENT * EXTENT)
    windings = jnp.stack(
        [
            (step_x * coord_x + step_y * coord_y + step_z * coord_z) % EXTENT
            for step_x, step_y, step_z in MOMENTA
        ]
    )
    angles = windings.astype(jnp.float32) * (2.0 * math.pi / EXTENT)
    return (jnp.cos(angles), jnp.sin(angles))


def phased_rows(prop_colour, cosine_table, sine_table):
    real_part = prop_colour[0].astype(jnp.float32)[None]
    imag_part = prop_colour[1].astype(jnp.float32)[None]
    cos_rows = cosine_table[:, None, None, :]
    sin_rows = sine_table[:, None, None, :]
    turned = jnp.stack(
        [cos_rows * real_part + sin_rows * imag_part, cos_rows * imag_part - sin_rows * real_part]
    )
    return turned.astype(jnp.bfloat16).reshape(-1, turned.shape[-1])


def project(eig_colour, phased, scale_in):
    site_dims = (((1,), (1,)), ((), ()))
    from_real = lax.dot_general(
        eig_colour[0], phased, site_dims, preferred_element_type=jnp.float32
    ).reshape(-1, 2, NMOM, 48)
    from_imag = lax.dot_general(
        eig_colour[1], phased, site_dims, preferred_element_type=jnp.float32
    ).reshape(-1, 2, NMOM, 48)
    real_part = from_real[:, 0] + from_imag[:, 1]
    imag_part = from_real[:, 1] - from_imag[:, 0]
    return jnp.stack([real_part, imag_part]) * scale_in


def assemble(pieces):
    stacked = jnp.stack(pieces)
    vectors = stacked.shape[2]
    return stacked.transpose(3, 1, 2, 0, 4).reshape(NMOM, 2, vectors, 144)


def weighted_total(blocks, weights):
    real_sum = jnp.einsum("k,pkc->pc", weights[0], blocks[:, 0], precision=PRECISE) - jnp.einsum(
        "k,pkc->pc", weights[1], blocks[:, 1], precision=PRECISE
    )
    imag_sum = jnp.einsum("k,pkc->pc", weights[0], blocks[:, 1], precision=PRECISE) + jnp.einsum(
        "k,pkc->pc", weights[1], blocks[:, 0], precision=PRECISE
    )
    return jnp.stack([real_sum, imag_sum], axis=1)


def term_tables(term_index, term_sign):
    channels = jnp.arange(12, dtype=jnp.int32)
    first_pick = (term_index[:, 0:1] == channels[None]).astype(jnp.float32)
    second_pick = (term_index[:, 1:2] == channels[None]).astype(jnp.float32)
    sign_values = (2 * term_sign - 1).astype(jnp.float32)
    placement = (term_index[None, :, 2] == channels[:, None]).astype(jnp.float32) * sign_values[
        None
    ]
    return (first_pick, second_pick, placement)


def contract(blocks, weighted, first_pick, second_pick, placement):
    vectors = blocks.shape[2]
    block_grid = blocks.reshape(NMOM, 2, vectors, 12, 12)
    first_terms = jnp.einsum("mi,pqkij->pqkmj", first_pick, block_grid, precision=PRECISE)
    second_terms = jnp.einsum(
        "mi,pqij->pqmj", second_pick, weighted.reshape(NMOM, 2, 12, 12), precision=PRECISE
    )[:, :, None]
    real_part = first_terms[:, 0] * second_terms[:, 0] - first_terms[:, 1] * second_terms[:, 1]
    imag_part = first_terms[:, 0] * second_terms[:, 1] + first_terms[:, 1] * second_terms[:, 0]
    product = jnp.stack([real_part, imag_part], axis=1)
    return jnp.einsum("cm,pqkmj->pqkcj", placement, product, precision=PRECISE).reshape(
        NMOM, 2, vectors, 144
    )


def rebuild(coeffs, eig_colour, colour, cosine_table, sine_table, scale_out):
    vectors = coeffs.shape[2]
    colour_block = coeffs.reshape(NMOM, 2, vectors, 3, 48)[:, :, :, colour]
    coeff_table = colour_block.transpose(2, 1, 0, 3).reshape(vectors, 2 * NMOM * 48)
    vector_dims = (((0,), (0,)), ((), ()))
    from_real = lax.dot_general(
        coeff_table, eig_colour[0], vector_dims, preferred_element_type=jnp.float32
    ).reshape(2, NMOM, 48, -1)
    from_imag = lax.dot_general(
        coeff_table, eig_colour[1], vector_dims, preferred_element_type=jnp.float32
    ).reshape(2, NMOM, 48, -1)
    real_part = from_real[0] - from_imag[1]
    imag_part = from_real[1] + from_imag[0]
    cos_rows = cosine_table[:, None, :]
    sin_rows = sine_table[:, None, :]
    out_real = jnp.sum(cos_rows * real_part - sin_rows * imag_part, axis=0)
    out_imag = jnp.sum(cos_rows * imag_part + sin_rows * real_part, axis=0)
    return jnp.stack([out_real, out_imag]) * scale_out


def on_device(
    propagator, eigvecs, operator_weights, sink_time, term_index, term_sign, solver_order
):
    length = propagator.shape[-1]
    devices = lax.axis_size(SPACE)
    offset = lax.axis_index(SPACE) * length
    cosine_table, sine_table = phase_tables(offset, length)
    scale_in = 1.0 / math.sqrt(3.0 * length * devices)
    pieces = []
    for colour in range(3):
        phased = phased_rows(propagator[:, colour], cosine_table, sine_table)
        pieces.append(project(eigvecs[:, colour], phased, scale_in))
    partial_blocks = assemble(pieces)
    weights = lax.dynamic_index_in_dim(operator_weights, sink_time[0], 0, keepdims=False)
    first_pick, second_pick, placement = term_tables(term_index, term_sign)
    blocks = sum_all_axes(partial_blocks, SPACE)
    weighted = weighted_total(blocks, weights)
    coeffs = contract(blocks, weighted, first_pick, second_pick, placement).astype(jnp.bfloat16)
    scale_out = 1.0 / math.sqrt(NMOM * NVEC)
    colours = [
        rebuild(coeffs, eigvecs[:, colour], colour, cosine_table, sine_table, scale_out)
        for colour in range(3)
    ]
    source = jnp.stack(colours, axis=1).astype(jnp.bfloat16).reshape(2 * 3 * 48, length)
    wanted = core_and_chips(solver_order.reshape(devices, -1), ("space_0", "space_1"), (1, 0), 0, 0)
    local_index = wanted.reshape(length) - offset
    picked = jnp.take(source, local_index, axis=1)
    placed = core_and_chips(picked, ("space_0", "space_1"), (1, 0), 1, 1)
    return placed.reshape(2, 3, 4, 12, length)


def solution(mesh):
    finer = Mesh(mesh.devices.reshape(mesh.shape["grp"], 32, 2), ("grp", "space_0", "space_1"))
    in_specs = (
        P("grp", None, None, None, SPACE),
        P("grp", None, None, SPACE),
        P("grp", None, None),
        P("grp"),
        P(),
        P(),
        P(SPACE),
    )
    out_specs = P("grp", None, None, None, SPACE)
    return jax.shard_map(
        on_device, mesh=finer, in_specs=in_specs, out_specs=out_specs, check_vma=False
    )
```

profile of v0, /device:TPU:37, one launch (start us, length us, event | category | flops | bytes accessed | tf_op | source)
XLA Modules:
  0.0 657.9 jit_solution(16684948482462096606)
XLA Ops:
  10.1 2.8 add_convert_fusion.2
  14.5 3.2 fusion.33
  17.7 2.7 fusion.29
  22.1 3.2 fusion.25
  25.2 2.7 fusion.21
  29.6 2.4 fusion.17
  40.3 23.8 %all_to_all.20 = s32[2,1,1024]{2,1,0:T(1,128)S(1)} all-to-all(s32[2,1,1024]{2,1,0:T(1,128)S(1)} %reshape.984), channel_id=1, replica_groups=mesh['grp'=4,'space_0'=32,'space_1'=2] {'space_1'}, dimensions={0} | all-to-all | bytes 16384 | tf_op jit(solution)/shard_map/all_to_all | solution.py:72
  65.9 13.4 %all-to-all-start.1 = ((s32[32,2,1,32]{3,1,2,0:T(2,128)}), s32[32,2,1,32]{3,1,2,0:T(2,128)S(1)}, u32[]{:S(2)}, u32[]{:S(2)}) async-start(s32[32,2,1,32]{3,1,2,0:T(2,128)} %copy.108), calls=%async_computation.1 | async-start | bytes 65536 | tf_op jit(solution)/shard_map/all_to_all | solution.py:72
  81.2 19.1 %all-to-all-done.1 = s32[32,2,1,32]{3,1,2,0:T(2,128)S(1)} async-done(((s32[32,2,1,32]{3,1,2,0:T(2,128)}), s32[32,2,1,32]{3,1,2,0:T(2,128)S(1)}, u32[]{:S(2)}, u32[]{:S(2)}) %all-to-all-start.1) | async-done | bytes 8224 | tf_op jit(solution)/shard_map/all_to_all | solution.py:72
  100.4 60.1 %reduce-scatter.5.cloned.1.call-done = f32[2,16,144]{2,1,0:T(8,128)} async-done(((f32[64,16,144]{2,1,0:T(8,128)}), f32[2,16,144]{2,1,0:T(8,128)}) %reduce-scatter.5.cloned.1.call-update) | async-done | bytes 18448 | tf_op jit(solution)/shard_map/reduce_scatter | solution.py:31
  160.8 47.2 %reduce-scatter.9.cloned.1.call-done = f32[32,16,144]{2,1,0:T(8,128)} async-done(((f32[64,16,144]{2,1,0:T(8,128)}), f32[32,16,144]{2,1,0:T(8,128)}) %reduce-scatter.9.cloned.1.call-update) | async-done | bytes 294928 | tf_op jit(solution)/shard_map/reduce_scatter | solution.py:31
  208.1 28.2 %reduce-scatter.7.cloned.1.call-done = f32[1,16,144]{2,1,0:T(8,128)} async-done(((f32[2,16,144]{2,1,0:T(8,128)}), f32[1,16,144]{2,1,0:T(8,128)}) %reduce-scatter.7.cloned.1.call-update) | async-done | bytes 9232 | tf_op jit(solution)/shard_map/reduce_scatter | solution.py:31
  236.3 2.1 all_gather.18
  238.4 50.6 %all-gather = f32[64,16,144]{2,1,0:T(8,128)S(1)} all-gather(f32[2,16,144]{2,1,0:T(8,128)S(1)} %all_gather.18), channel_id=2, replica_groups=mesh['grp'=4,'space_0'=32,'space_1'=2] {'space_0'}, dimensions={0}, use_global_device_ids=true | all-gather | bytes 608256 | tf_op jit(solution)/shard_map/all_gather | solution.py:38
  289.0 57.5 %reduce-scatter.11.cloned.1.call-done = f32[1,16,144]{2,1,0:T(8,128)} async-done(((f32[32,16,144]{2,1,0:T(8,128)}), f32[1,16,144]{2,1,0:T(8,128)}) %reduce-scatter.11.cloned.1.call-update) | async-done | bytes 9232 | tf_op jit(solution)/shard_map/reduce_scatter | solution.py:31
  346.5 42.8 %all_gather.21 = f32[32,16,144]{2,1,0:T(8,128)S(1)} all-gather(f32[1,16,144]{2,1,0:T(8,128)} %reduce-scatter.11.cloned.1.call-done), channel_id=1, replica_groups=mesh['grp'=4,'space_0'=32,'space_1'=2] {'space_0'}, dimensions={0}, use_global_device_ids=true | all-gather | bytes 304128 | tf_op jit(solution)/shard_map/all_gather | solution.py:38
  389.3 38.6 %all-gather.1 = f32[64,16,144]{2,1,0:T(8,128)S(1)} all-gather(f32[32,16,144]{2,1,0:T(8,128)S(1)} %all_gather.21), channel_id=3, replica_groups=mesh['grp'=4,'space_0'=32,'space_1'=2] {'space_1'}, dimensions={0}, use_global_device_ids=true | all-gather | bytes 884736 | tf_op jit(solution)/shard_map/all_gather | solution.py:38
  435.4 2.6 convolution_bitcast_fusion
  439.1 2.5 fusion.8
  451.1 7.5 %gather_fusion = bf16[2048,288]{1,0:T(8,128)(2,1)S(1)} fusion(bf16[288,2048]{0,1:T(8,128)(2,1)S(1)} %copy.130, s32[2048]{0:T(1024)S(1)} %broadcast_clamp_fusion), kind=kCustom, calls=%fused_computation | custom fusion | bytes 2367488 | tf_op jit(solution)/shard_map/jit(_take)/gather | solution.py:209
  459.2 5.0 all_to_all.21
  464.5 172.4 %all_to_all.22 = bf16[32,2,288,32]{2,3,1,0:T(8,128)(2,1)S(1)} all-to-all(bf16[32,2,288,32]{2,3,1,0:T(8,128)(2,1)S(1)} %copy.132), channel_id=1, replica_groups=mesh['grp'=4,'space_0'=32,'space_1'=2] {'space_0'}, dimensions={0} | all-to-all | bytes 2359296 | tf_op jit(solution)/shard_map/all_to_all | solution.py:72
  637.0 5.4 copy.133
  642.4 7.0 %reshape_reshape.15 = bf16[2,3,4,12,2048]{4,3,2,1,0:T(8,128)(2,1)S(1)} reshape(bf16[288,64,32]{2,1,0:T(8,128)(2,1)} %bitcast.218) | data formatting | bytes 2359296 | tf_op jit(solution)/shard_map/reshape;reshape | solution.py:211
  (153 shorter events, 40.5 us)
Async XLA Ops:
  6.5 421.6 %copy-start = (f32[128,2,256]{2,1,0:T(2,128)S(1)}, f32[128,2,256]{2,1,0:T(2,128)}, u32[]{:S(2)}) copy-start(f32[128,2,256]{2,1,0:T(2,128)} %param.9) | copy-start | bytes 786436
  6.6 153.9 %reduce-scatter.5.cloned.1.call-start = ((), (), s32[]{:S(2)}) async-start(), calls=%async_computation.8 | async-start | bytes 1081344 | tf_op jit(solution)/shard_map/reduce_scatter | solution.py:31
  10.1 2.8 copy-start.12
  10.1 2.8 copy-start.14
  14.5 3.2 copy-start.5
  17.7 2.7 copy-start.3
  17.7 2.7 copy-start.4
  22.1 3.2 copy-start.6
  25.2 2.7 copy-start.2
  29.6 2.4 copy-start.7
  32.0 2.0 copy-start.10
  32.0 2.0 copy-start.11
  32.0 2.1 copy-start.8
  32.0 2.1 copy-start.9
  37.1 170.9 %reduce-scatter.9.cloned.1.call-start = ((), (), s32[]{:S(2)}) async-start(), calls=%async_computation.10 | async-start | bytes 1572864 | tf_op jit(solution)/shard_map/reduce_scatter | solution.py:31
  38.9 40.4 %copy-start.24 = (s32[48,3]{0,1:T(4,128)S(1)}, s32[48,3]{0,1:T(4,128)}, u32[]{:S(2)}) copy-start(s32[48,3]{0,1:T(4,128)} %param.11) | copy-start | bytes 1732
  38.9 41.0 %copy-start.26 = (s32[48]{0:T(128)S(1)}, s32[48]{0:T(128)}, u32[]{:S(2)}) copy-start(s32[48]{0:T(128)} %param.12) | copy-start | bytes 580
  65.9 34.4 %all-to-all-start.1 = ((s32[32,2,1,32]{3,1,2,0:T(2,128)}), s32[32,2,1,32]{3,1,2,0:T(2,128)S(1)}, u32[]{:S(2)}, u32[]{:S(2)}) async-start(s32[32,2,1,32]{3,1,2,0:T(2,128)} %copy.108), calls=%async_computation.1 | async-start | bytes 65536 | tf_op jit(solution)/shard_map/all_to_all | solution.py:72
  79.3 157.0 %reduce-scatter.7.cloned.1.call-start = ((), (), s32[]{:S(2)}) async-start(), calls=%async_computation.9 | async-start | bytes 49152 | tf_op jit(solution)/shard_map/reduce_scatter | solution.py:31
  160.5 186.0 %reduce-scatter.11.cloned.1.call-start = ((), (), s32[]{:S(2)}) async-start(), calls=%async_computation.11 | async-start | bytes 540672 | tf_op jit(solution)/shard_map/reduce_scatter | solution.py:31
  433.7 1.6 copy-start.22
  435.4 7.4 %slice-start = ((s8[6291456]{0:T(1024)(128)(4,1)}), s8[4194304]{0:T(1024)(128)(4,1)S(1)}, s32[]{:S(2)}) async-start(s8[6291456]{0:T(1024)(128)(4,1)} %bitcast.227), calls=%async_computation.12 | async-start | bytes 8388608
  438.0 4.8 slice-start.1
  642.4 9.0 %copy-start.1 = (f32[128,2,256]{2,1,0:T(2,128)S(1)}, f32[128,2,256]{2,1,0:T(2,128)}, u32[]{:S(2)}) copy-start(f32[128,2,256]{2,1,0:T(2,128)} %param.9) | copy-start | bytes 786436
  (10 other events, 9.8 us)
Sparse Core Ops, SparseCore 0:
  37.3 123.1 reduce-scatter.4
  163.0 45.0 reduce-scatter.8
  210.5 25.7 reduce-scatter.6
  238.7 107.7 reduce-scatter.10
where the time goes:
time: 659 us; the launch traced here: 658 us
  blocking collectives  335 us (51%)
  waiting for transfers between devices  212 us (32%)
  local copies, waits for them, and re-layouts  39.6 us (6%)
  matrix products  29.7 us (5%)
  between operations  14.6 us (2%)
  starting transfers between devices  13.8 us (2%)
  other arithmetic  12.6 us (2%)
    all_to_all x3, blocking collectives, exchange_in_order(): lax.all_to_all(blocks, axes[k], split_axis=k, concat_axis=k, tiled=True)  201 us
    reduce_scatter x4, waiting for transfers between devices, own_block(): blocks = lax.psum_scatter(blocks, axes[k], scatter_dimension=0, tiled=True)  193 us
    all_gather x4, blocking collectives, all_blocks(): blocks = lax.all_gather(blocks, axes[k])  134 us
    all_to_all x1, waiting for transfers between devices, exchange_in_order(): lax.all_to_all(blocks, axes[k], split_axis=k, concat_axis=k, tiled=True)  19.1 us
    all_to_all x1, starting transfers between devices, exchange_in_order(): lax.all_to_all(blocks, axes[k], split_axis=k, concat_axis=k, tiled=True)  13.4 us
  transfers between devices with their start and end apart: 5, of which 5 were waited for; matrix products, arithmetic and copies ran while one was open for 1% of the time, Pallas kernels for 0%

commit v1 on v0

v1 whole, which is shorter than its diff:
```python
import functools
import math

import jax
import jax.numpy as jnp
import ml_dtypes
import numpy as np
from jax import lax
from jax.experimental import pallas as pl
from jax.experimental.pallas import tpu as pltpu
from jax.sharding import Mesh
from jax.sharding import PartitionSpec as P

NVEC = 256
NMOM = 4
NTERM = 48
EXTENT = 64
SPACE = ("space_0", "space_1")
MESH = pl.DeviceIdType.MESH
PRECISE = lax.Precision.HIGHEST
F32 = jnp.float32
BF16 = jnp.bfloat16

LANES = 128
HALF = 24
CHUNK = 512
GROUP = 256


def fixed_tables(length, chips):
    assert 2 * length == EXTENT * EXTENT
    site = np.arange(length)
    turn = 2.0 * np.pi / EXTENT
    angle_x = turn * (site % EXTENT)
    tables, pieces = [], []
    for core in range(2):
        angle_y = turn * ((core * length + site) // EXTENT % EXTENT)
        rows = np.stack([np.cos(angle_x), np.sin(angle_x), np.cos(angle_y), np.sin(angle_y)]).astype(np.float32)
        tables.append(np.concatenate([rows, np.zeros_like(rows)]))
        high = rows.astype(ml_dtypes.bfloat16)
        middle = (rows - high.astype(np.float32)).astype(ml_dtypes.bfloat16)
        low = (rows - high.astype(np.float32) - middle.astype(np.float32)).astype(ml_dtypes.bfloat16)
        pieces.append(np.concatenate([high, middle, low, np.zeros_like(high)]))
    angle_z = turn * (np.arange(chips) % EXTENT)
    chip_phase = np.zeros((chips, 8, LANES), np.float32)
    chip_phase[:, 0] = np.cos(angle_z)[:, None]
    chip_phase[:, 1] = np.sin(angle_z)[:, None]
    pick = np.zeros((2, 8, 512), np.float32)
    fold = np.zeros((2, 512, LANES), np.float32)
    for colour in range(3):
        for row in range(6):
            for u in range(HALF):
                lane = colour * 144 + row * HALF + u
                pick[0, row, lane] = 1.0
                pick[1, row ^ 1, lane] = 1.0 if row % 2 == 0 else -1.0
                fold[0, lane, colour * HALF + u] = 1.0
                fold[1, lane, 48 + colour * HALF + u] = 1.0
    return np.stack(tables), np.stack(pieces), chip_phase, pick, fold


def term_matrices(term_index, term_sign):
    row = jnp.arange(LANES, dtype=jnp.int32)[:, None]
    lane = jnp.arange(384, dtype=jnp.int32)[None]
    spread = jnp.pad(jnp.repeat(term_index.T, 6, axis=1), ((0, 0), (0, 384 - 288)), constant_values=-1)
    signs = jnp.pad(jnp.repeat((2 * term_sign - 1).astype(F32), 6), (0, 384 - 288))
    same = (row % 6 == lane % 6) & (row < 72)
    first = jnp.where(same & (row // 6 == spread[0][None]), 1.0, 0.0)
    second = jnp.where(same & (row // 6 == spread[1][None]), 1.0, 0.0)
    place = jnp.where(same & (row // 6 == spread[2][None]), signs[None], 0.0)
    return jnp.stack([first, second, place]).astype(F32)


def dot(a, b, precision=None):
    return lax.dot_general(a, b, (((1,), (0,)), ((), ())), preferred_element_type=F32, precision=precision)


def dot_nt(a, b, precision=None):
    return lax.dot_general(a, b, (((1,), (1,)), ((), ())), preferred_element_type=F32, precision=precision)


def far_first(step, count):
    half = (step + 1) // 2
    return count // 2 + half * (1 - 2 * (step % 2))


def swap_blocks(tiles, lane_block):
    result = []
    for g in range(4):
        message = tiles[0] if g == 0 else pltpu.roll(tiles[0], (-g * 32) % LANES, 1)
        for q in range(1, 4):
            moved = tiles[q] if q == g else pltpu.roll(tiles[q], ((q - g) * 32) % LANES, 1)
            message = jnp.where(lane_block == q, moved, message)
        result.append(message)
    return result


def lane_blocks():
    return lax.broadcasted_iota(jnp.int32, (72, LANES), 1) // 32


def whole_kernel(
    chips, length, scale_in, scale_out,
    eig, prop, idx_rows, weights, tables, pieces, chip_phase, pick, fold, terms,
    out,
    eig_v, prop_v, accs, full, from_core, chip_sum, rs_send, rs_recv, idx_recv,
    perm, eig_p, phase_p, gathered, coeff_t, left, source, to_send,
    load_sem, core_sem, idx_sem, rs_sem, near_sem, ag_sem, side_sem, both_sem, all_sem,
):
    z = lax.axis_index("space_0")
    core = lax.axis_index("space_1")
    devices = 2 * chips
    me = 2 * z + core
    other = 1 - core

    def device(chip, on_core):
        return {"space_0": chip, "space_1": on_core}

    def remote(src, dst, send_sem, recv_sem, chip, on_core):
        return pltpu.make_async_remote_copy(
            src_ref=src, dst_ref=dst, send_sem=send_sem, recv_sem=recv_sem,
            device_id=device(chip, on_core), device_id_type=MESH,
        )

    loads = []
    for a in range(3):
        for q in range(2):
            loads.append(pltpu.make_async_copy(prop.at[q, a], prop_v.at[q, a], load_sem.at[4 * a + q]))
            loads.append(pltpu.make_async_copy(eig.at[q, a], eig_v.at[a, pl.ds(q * NVEC, NVEC)], load_sem.at[4 * a + 2 + q]))
    for load in loads:
        load.start()

    barrier = pltpu.get_barrier_semaphore()

    def greet(i, carry):
        peer = lax.rem(me + i, devices)
        pl.semaphore_signal(barrier, inc=1, device_id=device(peer // 2, lax.rem(peer, 2)), device_id_type=MESH)
        return carry

    lax.fori_loop(1, devices, greet, 0)

    for a in range(3):
        for load in loads[4 * a : 4 * a + 4]:
            load.wait()
        for h in range(2):
            accs[h, a] = jnp.zeros((NVEC, 144), F32)

        def project(ci, carry, a=a):
            sites = pl.ds(pl.multiple_of(ci * CHUNK, CHUNK), CHUNK)
            table = tables[core, :, sites]
            cos_x, sin_x, cos_y, sin_y = (table[n : n + 1] for n in range(4))
            real = prop_v[0, a, :, :, sites].astype(F32)
            imag = prop_v[1, a, :, :, sites].astype(F32)
            for h in range(2):
                re = jnp.concatenate([real[s, 6 * h : 6 * h + 6] for s in range(4)], axis=0)
                im = jnp.concatenate([imag[s, 6 * h : 6 * h + 6] for s in range(4)], axis=0)
                re_x, im_x = cos_x * re + sin_x * im, cos_x * im - sin_x * re
                re_y, im_y = cos_y * re + sin_y * im, cos_y * im - sin_y * re
                with_real = jnp.concatenate([re, im, re_x, im_x, re_y, im_y], axis=0).astype(BF16)
                with_imag = jnp.concatenate([im, -re, im_x, -re_x, im_y, -re_y], axis=0).astype(BF16)
                accs[h, a] += dot_nt(eig_v[a, 0:NVEC, sites], with_real) + dot_nt(eig_v[a, NVEC : 2 * NVEC, sites], with_imag)
            return carry

        lax.fori_loop(0, length // CHUNK, project, 0)

    def join_colours(rb, carry):
        rows = pl.ds(pl.multiple_of(rb * 32, 32), 32)
        for h in range(2):
            full[h, rows] = jnp.concatenate([accs[h, a, rows] for a in range(3)] + [jnp.zeros((32, 80), F32)], axis=1)
        return carry

    lax.fori_loop(0, NVEC // 32, join_colours, 0)

    pl.semaphore_wait(barrier, devices - 1)

    to_core = remote(full.at[other], from_core, core_sem.at[0], core_sem.at[1], z, other)
    to_core.start()

    def send_index(i, carry):
        peer = lax.rem(me + far_first(i, devices), devices)
        remote(idx_rows.at[peer], idx_recv.at[me], idx_sem.at[0], idx_sem.at[1], peer // 2, lax.rem(peer, 2)).start()
        return carry

    lax.fori_loop(0, devices - 1, send_index, 0)
    idx_recv[me] = idx_rows[me]

    to_core.wait()
    chip_sum[...] = (full[core] + from_core[...]) * scale_in

    by_weight = dot(weights[...], chip_sum[...], PRECISE)
    weighted_rows = by_weight[0:1] * pick[0] + by_weight[1:2] * pick[1]
    weighted_part = dot(weighted_rows, fold[1], PRECISE)
    beside = jnp.concatenate([jnp.zeros((8, 384), F32), weighted_part], axis=1)

    def pack(zz, carry):
        rows = pl.ds(pl.multiple_of(zz * 8, 8), 8)
        rs_send[zz] = (chip_sum[rows] + beside).astype(BF16)
        return carry

    lax.fori_loop(0, chips, pack, 0)

    def send_part(i, carry):
        peer = lax.rem(z + far_first(i, chips), chips)
        remote(rs_send.at[peer], rs_recv.at[z], rs_sem.at[0], rs_sem.at[1], peer, core).start()
        return carry

    lax.fori_loop(0, chips - 1, send_part, 0)
    rs_recv[z] = rs_send[z]

    some = pl.ds(0, devices - 1)
    pltpu.make_async_copy(idx_recv.at[some], idx_recv.at[some], idx_sem.at[1]).wait()

    def reorder(g, carry):
        columns = pl.ds(pl.multiple_of(g * GROUP, GROUP), GROUP)
        wanted = jnp.concatenate(
            [sum(idx_recv[g * 8 + 4 * k + n] for n in range(4)) for k in range(2)], axis=1
        ) - me * length

        def one_hot(rb, inner):
            rows = pl.ds(pl.multiple_of(rb * 64, 64), 64)
            here = lax.broadcasted_iota(jnp.int32, (64, GROUP), 0) + rb * 64
            perm[rows] = jnp.where(here == wanted, 1.0, 0.0).astype(BF16)
            return inner

        lax.fori_loop(0, length // 64, one_hot, 0)
        for a in range(3):
            eig_p[a, :, columns] = dot(eig_v[a], perm[...]).astype(BF16)
        turned = dot(pieces[core], perm[...])
        phase_p[:, columns] = jnp.concatenate([turned[0:4] + turned[4:8] + turned[8:12], jnp.zeros((4, GROUP), F32)], axis=0)
        return carry

    lax.fori_loop(0, length // GROUP, reorder, 0)

    some = pl.ds(0, chips - 1)
    pltpu.make_async_copy(rs_recv.at[some], rs_recv.at[some], rs_sem.at[1]).wait()
    total = jnp.zeros((8, 512), F32)
    total_cos = jnp.zeros((8, 512), F32)
    total_sin = jnp.zeros((8, 512), F32)
    for zz in range(chips):
        part = rs_recv[zz].astype(F32)
        total = total + part
        total_cos = total_cos + chip_phase[zz, 0:1, 0:1] * part
        total_sin = total_sin + chip_phase[zz, 1:2, 0:1] * part
    masks = pick[0]
    blocks = [total * masks[r : r + 1] for r in range(6)]
    blocks.append(total_cos * masks[0:1] + total_sin * masks[1:2])
    blocks.append(total_cos * masks[1:2] - total_sin * masks[0:1])
    block_rows = dot(jnp.concatenate(blocks, axis=0), fold[0], PRECISE)
    tails = [pltpu.roll(t[:, 384:512], LANES - 48, 1) for t in (total, total_cos, total_sin)]
    weighted = jnp.concatenate(
        [tails[0][0:6], tails[1][0:1] + tails[2][1:2], tails[1][1:2] - tails[2][0:1]], axis=0
    )
    first = dot(block_rows, terms[0], PRECISE)
    second = dot(weighted, terms[1], PRECISE)
    products = []
    for p in range(NMOM):
        first_re, first_im = first[16 * p : 16 * p + 8], first[16 * p + 8 : 16 * p + 16]
        second_re, second_im = second[2 * p : 2 * p + 1], second[2 * p + 1 : 2 * p + 2]
        products.append(first_re * second_re - first_im * second_im)
        products.append(first_re * second_im + first_im * second_re)
    coeffs = dot_nt(jnp.concatenate(products, axis=0), terms[2], PRECISE)
    piece = jnp.concatenate([coeffs[8 * b : 8 * b + 8, 0:72] for b in range(8)] + [jnp.zeros((8, 64), F32)], axis=1)
    parity, pair = lax.rem(z, 2), z // 2
    pairs = chips // 2
    beside_z = z + 1 - 2 * parity
    gathered[core, parity, pair] = piece.astype(BF16)

    def send_far(i, carry):
        peer = lax.rem(pair + far_first(i, pairs), pairs)
        mine = gathered.at[core, parity, pair]
        remote(mine, mine, near_sem.at[0], ag_sem.at[pair], 2 * peer + parity, core).start()
        return carry

    lax.fori_loop(0, pairs - 1, send_far, 0)
    mine = gathered.at[core, parity, pair]
    remote(mine, mine, near_sem.at[1], side_sem, beside_z, core).start()

    def hand_on(i, carry):
        peer = lax.rem(pair + far_first(i, pairs), pairs)
        came = gathered.at[core, parity, peer]
        pltpu.make_async_copy(came, came, ag_sem.at[peer]).wait()
        remote(came, came, near_sem.at[1], side_sem, beside_z, core).start()
        return carry

    lax.fori_loop(0, pairs - 1, hand_on, 0)
    own = gathered.at[core, parity]
    own_to_core = remote(own, own, both_sem.at[0], both_sem.at[1], z, other)
    own_to_core.start()
    theirs = gathered.at[core, 1 - parity]
    pltpu.make_async_copy(theirs, theirs, side_sem).wait()
    theirs_to_core = remote(theirs, theirs, both_sem.at[2], both_sem.at[3], z, other)
    theirs_to_core.start()
    own_to_core.wait_recv()
    theirs_to_core.wait_recv()

    for h in range(2):
        for lb in range(5):
            lanes = slice(lb * LANES, (lb + 1) * LANES)
            tall = jnp.concatenate([gathered[h, zz % 2, zz // 2, :, lanes].astype(F32) for zz in range(chips)], axis=0)
            coeff_t[h, lanes] = tall.T
    for a in range(3):
        def rows_of(q, sign=1.0):
            taken = [
                coeff_t[h, (2 * p + q) * 72 + a * HALF : (2 * p + q) * 72 + (a + 1) * HALF]
                for p in range(NMOM)
                for h in range(2)
            ]
            return (sign * jnp.concatenate(taken, axis=0)).astype(BF16)

        left[a, 0:192, 0:NVEC] = rows_of(0)
        left[a, 0:192, NVEC:] = rows_of(1, -1.0)
        left[a, 192:384, 0:NVEC] = rows_of(1)
        left[a, 192:384, NVEC:] = rows_of(0)

    cos_z, sin_z = chip_phase[z, 0:1, 0:1], chip_phase[z, 1:2, 0:1]
    groups = length // GROUP
    my_group = me // 8

    def rebuild(i, carry):
        g = lax.rem(my_group + jnp.where(i == groups - 1, 0, far_first(i, groups)), groups)
        columns = pl.ds(pl.multiple_of(g * GROUP, GROUP), GROUP)
        table = phase_p[:, columns]
        cos_x, sin_x, cos_y, sin_y = (table[n : n + 1] for n in range(4))
        for a in range(3):
            result = dot(left[a], eig_p[a, :, columns])
            re = [result[48 * p : 48 * p + 48] for p in range(NMOM)]
            im = [result[192 + 48 * p : 240 + 48 * p] for p in range(NMOM)]
            out_re = re[0] + (cos_x * re[1] - sin_x * im[1]) + (cos_y * re[2] - sin_y * im[2]) + (cos_z * re[3] - sin_z * im[3])
            out_im = im[0] + (cos_x * im[1] + sin_x * re[1]) + (cos_y * im[2] + sin_y * re[2]) + (cos_z * im[3] + sin_z * re[3])
            source[48 * a : 48 * a + 48] = out_re * scale_out
            source[144 + 48 * a : 192 + 48 * a] = out_im * scale_out
        for k in range(2):
            tiles = [source[72 * q : 72 * q + 72, k * LANES : (k + 1) * LANES] for q in range(4)]
            for n, message in enumerate(swap_blocks(tiles, lane_blocks())):
                to_send[g * 8 + 4 * k + n] = message.reshape(9, 8, LANES).astype(BF16)
        for n in range(8):
            peer = g * 8 + n

            @pl.when(peer != me)
            def _():
                remote(to_send.at[peer], out.at[me], all_sem.at[0], all_sem.at[1], peer // 2, lax.rem(peer, 2)).start()

        return carry

    lax.fori_loop(0, groups, rebuild, 0)
    keep = pltpu.make_async_copy(to_send.at[me], out.at[me], all_sem.at[2])
    keep.start()

    def drain(ref, sem):
        pltpu.make_async_copy(ref, ref, sem).wait()

    drain(idx_rows.at[pl.ds(0, devices - 1)], idx_sem.at[0])
    drain(rs_send.at[pl.ds(0, chips - 1)], rs_sem.at[0])
    drain(gathered.at[0, 0, pl.ds(0, pairs - 1)], near_sem.at[0])
    drain(gathered.at[0, 0], near_sem.at[1])
    own_to_core.wait_send()
    theirs_to_core.wait_send()
    drain(to_send.at[pl.ds(0, devices - 1)], all_sem.at[0])
    keep.wait()
    drain(out.at[pl.ds(0, devices - 1)], all_sem.at[1])


def format_kernel(inp, out):
    lane_block = lane_blocks()
    for k in range(inp.shape[0] // 4):
        tiles = [inp[4 * k + d].astype(F32).reshape(72, LANES) for d in range(4)]
        rows = jnp.concatenate(swap_blocks(tiles, lane_block), axis=0)
        for q in range(2):
            for a in range(3):
                base = q * 144 + a * 48
                for s in range(4):
                    low = rows[base + 6 * s : base + 6 * s + 6]
                    high = rows[base + HALF + 6 * s : base + HALF + 6 * s + 6]
                    out[q, a, s, :, k * LANES : (k + 1) * LANES] = jnp.concatenate([low, high], axis=0).astype(BF16)


def on_device(propagator, eigvecs, operator_weights, sink_time, term_index, term_sign, solver_order):
    length = propagator.shape[-1]
    chips = lax.axis_size("space_0")
    devices = lax.axis_size(SPACE)
    pair = length // devices
    scale_in = 1.0 / math.sqrt(3.0 * length * devices)
    scale_out = 1.0 / math.sqrt(NMOM * NVEC)
    tables, pieces, chip_phase, pick, fold = fixed_tables(length, chips)
    weights = lax.dynamic_index_in_dim(operator_weights, sink_time[0], 0, keepdims=False)
    weights = jnp.pad(weights, ((0, 6), (0, 0)))
    terms = term_matrices(term_index, term_sign)
    me = lax.axis_index(SPACE)
    lane = jnp.arange(LANES, dtype=jnp.int32)
    idx_rows = jnp.where(lane // pair == me % 4, jnp.tile(solver_order.reshape(devices, pair), (1, 4)), 0)
    idx_rows = idx_rows.reshape(devices, 1, LANES)

    vmem = pl.BlockSpec(memory_space=pltpu.VMEM)
    hbm = pl.BlockSpec(memory_space=pl.ANY)
    arrived = pl.pallas_call(
        functools.partial(whole_kernel, chips, length, scale_in, scale_out),
        out_shape=jax.ShapeDtypeStruct((devices, 9, 8, LANES), BF16),
        in_specs=[hbm, hbm] + [vmem] * 8,
        out_specs=hbm,
        scratch_shapes=[
            pltpu.VMEM((3, 2 * NVEC, length), BF16),
            pltpu.VMEM((2, 3, 4, 12, length), BF16),
            pltpu.VMEM((2, 3, NVEC, 144), F32),
            pltpu.VMEM((2, NVEC, 512), F32),
            pltpu.VMEM((NVEC, 512), F32),
            pltpu.VMEM((NVEC, 512), F32),
            pltpu.VMEM((chips, 8, 512), BF16),
            pltpu.VMEM((chips, 8, 512), BF16),
            pltpu.VMEM((devices, 1, LANES), jnp.int32),
            pltpu.VMEM((length, GROUP), BF16),
            pltpu.VMEM((3, 2 * NVEC, length), BF16),
            pltpu.VMEM((8, length), F32),
            pltpu.VMEM((2, 2, chips // 2, 8, 640), BF16),
            pltpu.VMEM((2, 640, NVEC), F32),
            pltpu.VMEM((3, 384, 2 * NVEC), BF16),
            pltpu.VMEM((288, GROUP), F32),
            pltpu.VMEM((devices, 9, 8, LANES), BF16),
            pltpu.SemaphoreType.DMA((12,)),
            pltpu.SemaphoreType.DMA((2,)),
            pltpu.SemaphoreType.DMA((2,)),
            pltpu.SemaphoreType.DMA((2,)),
            pltpu.SemaphoreType.DMA((2,)),
            pltpu.SemaphoreType.DMA((chips // 2,)),
            pltpu.SemaphoreType.DMA,
            pltpu.SemaphoreType.DMA((4,)),
            pltpu.SemaphoreType.DMA((3,)),
        ],
        compiler_params=pltpu.CompilerParams(collective_id=0, has_side_effects=True, vmem_limit_bytes=56 * 2**20),
    )(
        eigvecs, propagator, idx_rows, weights, jnp.asarray(tables), jnp.asarray(pieces),
        jnp.asarray(chip_phase), jnp.asarray(pick), jnp.asarray(fold), terms,
    )
    take = 16
    return pl.pallas_call(
        format_kernel,
        out_shape=jax.ShapeDtypeStruct((2, 3, 4, 12, length), BF16),
        grid=(devices // take,),
        in_specs=[pl.BlockSpec((take, 9, 8, LANES), lambda i: (i, 0, 0, 0))],
        out_specs=pl.BlockSpec((2, 3, 4, 12, take * pair), lambda i: (0, 0, 0, 0, i)),
    )(arrived)


def solution(mesh):
    finer = Mesh(mesh.devices.reshape(mesh.shape["grp"], -1, 2), ("grp", "space_0", "space_1"))
    in_specs = (
        P("grp", None, None, None, SPACE),
        P("grp", None, None, SPACE),
        P("grp", None, None),
        P("grp"),
        P(),
        P(),
        P(SPACE),
    )
    out_specs = P("grp", None, None, None, SPACE)
    return jax.shard_map(on_device, mesh=finer, in_specs=in_specs, out_specs=out_specs, check_vma=False)
```

time: 659 us -> 208 us (0.32)
  blocking collectives: 335 us -> 0 us
  waiting for transfers between devices: 212 us -> 0 us
  Pallas kernels: 0 us -> 196 us
  local copies, waits for them, and re-layouts: 39.6 us -> 7.84 us
  matrix products: 29.7 us -> 0 us
  starting transfers between devices: 13.8 us -> 0 us
  between operations: 14.6 us -> 0.85 us
  other arithmetic: 12.6 us -> 2.39 us
    all_to_all x3 -> x0, blocking collectives: 201 us -> none  [exchange_in_order(): lax.all_to_all(blocks, axes[k], split_axis=k, concat_axis=k, tiled=True)]
    pallas_call x0 -> x2, Pallas kernels: none -> 196 us  [the longest x1 192 us: on_device(): pl.pallas_call(functools.partial(whole_kernel, chips, length, scale_in, s...]
    reduce_scatter x4 -> x0, waiting for transfers between devices: 193 us -> none  [own_block(): blocks = lax.psum_scatter(blocks, axes[k], scatter_dimension=0, tiled=True)]
    all_gather x4 -> x0, blocking collectives: 134 us -> none  [all_blocks(): blocks = lax.all_gather(blocks, axes[k])]
    dot_general x19 -> x0, matrix products: 29.7 us -> none  [the longest x3 8.77 us: project(): lax.dot_general(eig_colour[0], phased, site_dims, preferred_element_type=...]
    all_to_all x1 -> x0, waiting for transfers between devices: 19.1 us -> none  [exchange_in_order(): lax.all_to_all(blocks, axes[k], split_axis=k, concat_axis=k, tiled=True)]
    all_to_all x1 -> x0, starting transfers between devices: 13.4 us -> none  [exchange_in_order(): lax.all_to_all(blocks, axes[k], split_axis=k, concat_axis=k, tiled=True)]
    another operation x12 -> x4, local copies, waits for them, and re-layouts: 12.9 us -> 0.91 us  [on_device(): jnp.tile(solver_order.reshape(devices, pair), (1, 4))]
  transfers between devices with their start and end apart: 5 -> 0, of which waited for: 5 -> 0; matrix products, arithmetic and copies ran while one was open for 1% -> 0% of each run, Pallas kernels for 0% -> 0%
where the time goes in v1:
time: 208 us
  Pallas kernels  196 us (94%)
  local copies, waits for them, and re-layouts  7.84 us (4%)
  other arithmetic  2.39 us (1%)
    pallas_call x1, Pallas kernels, on_device(): pl.pallas_call(functools.partial(whole_kernel, chips, length, scale_in, s...  192 us

profile of v1, /device:TPU:37, one launch (start us, length us, event | category | flops | bytes accessed | tf_op | source)
XLA Modules:
  0.0 207.6 jit_solution(5786816244919907657)
XLA Ops:
  0.0 0.0 copy-start
  0.0 0.0 copy-start.1
  0.8 0.7 add_convert_fusion
  1.5 0.0 copy-done
  1.5 0.6 pad.12.weights
  2.1 0.1 broadcast_in_dim.42
  2.2 0.1 reshape.456
  2.3 0.8 tile.10
  3.1 0.1 copy.15
  3.2 0.1 copy.16
  3.2 0.7 broadcast_select_fusion.idx_rows
  3.9 0.8 broadcast_in_dim.39
  4.7 0.1 reshape.455
  4.8 0.2 and_select_fusion.2
  5.0 0.9 pad_maximum_fusion.terms
  5.9 0.0 copy-done.1
  5.9 1.9 copy.17.prop
  7.7 192.3 %shard_map.118.inp = bf16[64,9,8,128]{3,2,1,0:T(8,128)(2,1)} custom-call(bf16[2,3,256,2048]{3,2,1,0:T(8,128)(2,1)} %eig.1, bf16[2,3,4,12,2048]{4,3,2,1,0:T(8,128)(2,1)} %copy.17.prop, s32[64,1,128]{2,1,0:T(1,128)} %broadcast_select_fusion.idx_rows, f32[8,256]{1,0:T(8,128)} %pad.12.weights, f32[2,8,2048]{2,1,0:T(8,128)} %constant.94.clone.tables, ...), custom_call_target="tpu_custom_call" | custom-call | tf_op jit(solution)/shard_map/pallas_call | solution.py:394
  200.1 4.1 %shard_map.119 = bf16[2,3,4,12,2048]{4,3,2,1,0:T(8,128)(2,1)} custom-call(bf16[64,9,8,128]{3,2,1,0:T(8,128)(2,1)} %shard_map.118.inp), custom_call_target="tpu_custom_call" | custom-call | tf_op jit(solution)/shard_map/pallas_call | solution.py:433
  204.2 3.3 %copy.18 = bf16[2,3,4,12,2048]{4,2,3,1,0:T(4,128)(2,1)} copy(bf16[2,3,4,12,2048]{4,3,2,1,0:T(8,128)(2,1)} %shard_map.119) | data formatting | bytes 2359296 | tf_op jit(solution)/shard_map/pallas_call | solution.py:433
  (8 shorter events, 0.1 us)
Async XLA Ops:
  0.0 1.5 copy-start
  0.0 5.9 %copy-start.1 = (bf16[2,3,4,12,2048]{4,2,3,1,0:T(4,128)(2,1)S(1)}, bf16[2,3,4,12,2048]{4,2,3,1,0:T(4,128)(2,1)}, u32[]{:S(2)}) copy-start(bf16[2,3,4,12,2048]{4,2,3,1,0:T(4,128)(2,1)} %param.12) | copy-start | bytes 3538948

commit v2 on v1

v2 whole, which is shorter than its diff:
```python
import functools
import math

import jax
import jax.numpy as jnp
import ml_dtypes
import numpy as np
from jax import lax
from jax.experimental import pallas as pl
from jax.experimental.pallas import tpu as pltpu
from jax.sharding import Mesh
from jax.sharding import PartitionSpec as P

NVEC = 256
NMOM = 4
NTERM = 48
EXTENT = 64
SPACE = ("space_0", "space_1")
MESH = pl.DeviceIdType.MESH
PRECISE = lax.Precision.HIGHEST
F32 = jnp.float32
BF16 = jnp.bfloat16

LANES = 128
HALF = 24
CHUNK = 512
GROUP = 256


def fixed_tables(length, chips):
    assert 2 * length == EXTENT * EXTENT
    site = np.arange(length)
    turn = 2.0 * np.pi / EXTENT
    angle_x = turn * (site % EXTENT)
    tables, pieces = [], []
    for core in range(2):
        angle_y = turn * ((core * length + site) // EXTENT % EXTENT)
        rows = np.stack([np.cos(angle_x), np.sin(angle_x), np.cos(angle_y), np.sin(angle_y)]).astype(np.float32)
        tables.append(np.concatenate([rows, np.zeros_like(rows)]))
        high = rows.astype(ml_dtypes.bfloat16)
        middle = (rows - high.astype(np.float32)).astype(ml_dtypes.bfloat16)
        low = (rows - high.astype(np.float32) - middle.astype(np.float32)).astype(ml_dtypes.bfloat16)
        pieces.append(np.concatenate([high, middle, low, np.zeros_like(high)]))
    angle_z = turn * (np.arange(chips) % EXTENT)
    chip_phase = np.zeros((chips, 8, LANES), np.float32)
    chip_phase[:, 0] = np.cos(angle_z)[:, None]
    chip_phase[:, 1] = np.sin(angle_z)[:, None]
    pick = np.zeros((2, 8, 512), np.float32)
    fold = np.zeros((2, 512, LANES), np.float32)
    for colour in range(3):
        for row in range(6):
            for u in range(HALF):
                lane = colour * 144 + row * HALF + u
                pick[0, row, lane] = 1.0
                pick[1, row ^ 1, lane] = 1.0 if row % 2 == 0 else -1.0
                fold[0, lane, colour * HALF + u] = 1.0
                fold[1, lane, 48 + colour * HALF + u] = 1.0
    return np.stack(tables), np.stack(pieces), chip_phase, pick, fold


def term_matrices(index, sign):
    shape = (LANES, 384)
    row = lax.broadcasted_iota(jnp.int32, shape, 0)
    column = lax.broadcasted_iota(jnp.int32, shape, 1) // 64
    same = (row % HALF // 4 == column) & (row < 72)
    channel = row // HALF * 4 + row % 4

    def along(values, rest):
        one = jnp.concatenate([values, jnp.full((1, 64 - NTERM), rest, values.dtype)], axis=1)
        return jnp.concatenate([one] * 6, axis=1)

    picks = [jnp.where(same & (channel == along(index[n : n + 1], -1)), 1.0, 0.0) for n in range(3)]
    signs = (2 * along(sign, 0) - 1).astype(F32)
    return picks[0], picks[1], picks[2] * signs


def dot(a, b, precision=None):
    return lax.dot_general(a, b, (((1,), (0,)), ((), ())), preferred_element_type=F32, precision=precision)


def dot_nt(a, b, precision=None):
    return lax.dot_general(a, b, (((1,), (1,)), ((), ())), preferred_element_type=F32, precision=precision)


def far_first(step, count):
    half = (step + 1) // 2
    return count // 2 + half * (1 - 2 * (step % 2))


def swap_blocks(tiles, lane_block):
    result = []
    for g in range(4):
        message = tiles[0] if g == 0 else pltpu.roll(tiles[0], (-g * 32) % LANES, 1)
        for q in range(1, 4):
            moved = tiles[q] if q == g else pltpu.roll(tiles[q], ((q - g) * 32) % LANES, 1)
            message = jnp.where(lane_block == q, moved, message)
        result.append(message)
    return result


def lane_blocks():
    return lax.broadcasted_iota(jnp.int32, (72, LANES), 1) // 32


def whole_kernel(
    chips, length, scale_in, scale_out,
    eig, prop, op_weights, sink, order, index, sign, tables, pieces, chip_phase, pick, fold,
    out,
    eig_v, prop_v, weights_v, sink_v, order_v, index_v, sign_v, tables_v, pieces_v, phase_v, pick_v, fold_v,
    accs, full, from_core, chip_sum, rs_send, rs_recv, idx_send, idx_recv, terms,
    perm, eig_p, phase_p, gathered, coeff_t, left, source, to_send, arrived, result,
    load_sem, table_sem, core_sem, idx_sem, rs_sem, near_sem, ag_sem, side_sem, both_send, both_sem, all_send, all_sem, out_sem,
):
    z = lax.axis_index("space_0")
    core = lax.axis_index("space_1")
    devices = 2 * chips
    me = 2 * z + core
    other = 1 - core

    def device(chip, on_core):
        return {"space_0": chip, "space_1": on_core}

    def remote(src, dst, send_sem, recv_sem, chip, on_core):
        return pltpu.make_async_remote_copy(
            src_ref=src, dst_ref=dst, send_sem=send_sem, recv_sem=recv_sem,
            device_id=device(chip, on_core), device_id_type=MESH,
        )

    loads = []
    for a in range(3):
        for q in range(2):
            loads.append(pltpu.make_async_copy(prop.at[q, a], prop_v.at[q, a], load_sem.at[4 * a + q]))
            loads.append(pltpu.make_async_copy(eig.at[q, a], eig_v.at[a, pl.ds(q * NVEC, NVEC)], load_sem.at[4 * a + 2 + q]))
    table_load = pltpu.make_async_copy(tables.at[core], tables_v, table_sem.at[0])
    late_loads = [
        pltpu.make_async_copy(op_weights, weights_v, table_sem.at[1]),
        pltpu.make_async_copy(pick, pick_v, table_sem.at[2]),
        pltpu.make_async_copy(fold, fold_v, table_sem.at[3]),
        pltpu.make_async_copy(pieces.at[core], pieces_v, table_sem.at[4]),
        pltpu.make_async_copy(chip_phase, phase_v, table_sem.at[5]),
        pltpu.make_async_copy(sink, sink_v, table_sem.at[6]),
        pltpu.make_async_copy(index, index_v, table_sem.at[7]),
        pltpu.make_async_copy(sign, sign_v, table_sem.at[8]),
        pltpu.make_async_copy(order, order_v, table_sem.at[9]),
    ]
    for load in [table_load] + loads + late_loads:
        load.start()

    barrier = pltpu.get_barrier_semaphore()

    def signal(chip, on_core):
        pl.semaphore_signal(barrier, inc=1, device_id=device(chip, on_core), device_id_type=MESH)

    def greet(i, carry):
        peer = lax.rem(z + far_first(i, chips), chips)
        signal(peer, 0)
        signal(peer, 1)
        return carry

    lax.fori_loop(0, chips - 1, greet, 0)
    signal(z, other)
    table_load.wait()

    for a in range(3):
        for load in loads[4 * a : 4 * a + 4]:
            load.wait()
        for h in range(2):
            accs[h, a] = jnp.zeros((NVEC, 144), F32)

        def project(ci, carry, a=a):
            sites = pl.ds(pl.multiple_of(ci * CHUNK, CHUNK), CHUNK)
            table = tables_v[:, sites]
            cos_x, sin_x, cos_y, sin_y = (table[n : n + 1] for n in range(4))
            real = prop_v[0, a, :, :, sites].astype(F32)
            imag = prop_v[1, a, :, :, sites].astype(F32)
            for h in range(2):
                re = real[6 * h : 6 * h + 6].reshape(HALF, CHUNK)
                im = imag[6 * h : 6 * h + 6].reshape(HALF, CHUNK)
                re_x, im_x = cos_x * re + sin_x * im, cos_x * im - sin_x * re
                re_y, im_y = cos_y * re + sin_y * im, cos_y * im - sin_y * re
                with_real = jnp.concatenate([re, im, re_x, im_x, re_y, im_y], axis=0).astype(BF16)
                with_imag = jnp.concatenate([im, -re, im_x, -re_x, im_y, -re_y], axis=0).astype(BF16)
                accs[h, a] += dot_nt(eig_v[a, 0:NVEC, sites], with_real) + dot_nt(eig_v[a, NVEC : 2 * NVEC, sites], with_imag)
            return carry

        lax.fori_loop(0, length // CHUNK, project, 0)

    def join_colours(rb, carry):
        rows = pl.ds(pl.multiple_of(rb * 32, 32), 32)
        for h in range(2):
            full[h, rows] = jnp.concatenate([accs[h, a, rows] for a in range(3)] + [jnp.zeros((32, 80), F32)], axis=1)
        return carry

    lax.fori_loop(0, NVEC // 32, join_colours, 0)

    for load in late_loads:
        load.wait()

    lane_block = lax.broadcasted_iota(jnp.int32, (devices // 4, LANES), 1) // 32
    my_block = lax.rem(me, 4)
    for k in range(4):
        moved = jnp.zeros((devices // 4, LANES), jnp.int32)
        for t in range(4):
            turned = order_v[...] if t == k else pltpu.roll(order_v[...], ((t - k) * 32) % LANES, 1)
            moved = jnp.where((lane_block == t) & (my_block == t), turned, moved)
        idx_send[k] = moved.reshape(devices // 4, 1, LANES)
    for n, matrix in enumerate(term_matrices(index_v[...], sign_v[...])):
        terms[n] = matrix
    pl.semaphore_wait(barrier, devices - 1)

    to_core = remote(full.at[other], from_core, core_sem.at[0], core_sem.at[1], z, other)
    to_core.start()

    def send_index(i, carry):
        peer = lax.rem(z + far_first(i, chips), chips)
        for n in range(2):
            mine = idx_send.at[2 * lax.rem(peer, 2) + n, peer // 2]
            remote(mine, idx_recv.at[me], idx_sem.at[0], idx_sem.at[1], peer, n).start()
        return carry

    lax.fori_loop(0, chips - 1, send_index, 0)
    remote(idx_send.at[2 * lax.rem(z, 2) + other, z // 2], idx_recv.at[me], idx_sem.at[0], idx_sem.at[1], z, other).start()
    idx_recv[me] = idx_send[my_block, z // 2]

    to_core.wait()
    chip_sum[...] = (full[core] + from_core[...]) * scale_in

    times = lax.broadcasted_iota(jnp.int32, weights_v.shape, 0)
    weights = jnp.sum(jnp.where(times == sink_v[...].reshape(1, 1, 1), weights_v[...], 0.0), axis=0)
    weights = jnp.concatenate([weights, jnp.zeros((6, NVEC), F32)], axis=0)
    by_weight = dot(weights, chip_sum[...], PRECISE)
    weighted_rows = by_weight[0:1] * pick_v[0] + by_weight[1:2] * pick_v[1]
    weighted_part = dot(weighted_rows, fold_v[1], PRECISE)
    beside = jnp.concatenate([jnp.zeros((8, 384), F32), weighted_part], axis=1)

    def pack(zz, carry):
        rows = pl.ds(pl.multiple_of(zz * 8, 8), 8)
        rs_send[zz] = (chip_sum[rows] + beside).astype(BF16)
        return carry

    lax.fori_loop(0, chips, pack, 0)

    def send_part(i, carry):
        peer = lax.rem(z + far_first(i, chips), chips)
        remote(rs_send.at[peer], rs_recv.at[z], rs_sem.at[0], rs_sem.at[1], peer, core).start()
        return carry

    lax.fori_loop(0, chips - 1, send_part, 0)
    rs_recv[z] = rs_send[z]

    some = pl.ds(0, devices - 1)
    pltpu.make_async_copy(idx_recv.at[some], idx_recv.at[some], idx_sem.at[1]).wait()

    def reorder(g, carry):
        columns = pl.ds(pl.multiple_of(g * GROUP, GROUP), GROUP)
        wanted = jnp.concatenate(
            [sum(idx_recv[g * 8 + 4 * k + n] for n in range(4)) for k in range(2)], axis=1
        ) - me * length

        def one_hot(rb, inner):
            rows = pl.ds(pl.multiple_of(rb * 64, 64), 64)
            here = lax.broadcasted_iota(jnp.int32, (64, GROUP), 0) + rb * 64
            perm[rows] = jnp.where(here == wanted, 1.0, 0.0).astype(BF16)
            return inner

        lax.fori_loop(0, length // 64, one_hot, 0)
        for a in range(3):
            eig_p[a, :, columns] = dot(eig_v[a], perm[...]).astype(BF16)
        turned = dot(pieces_v[...], perm[...])
        phase_p[:, columns] = jnp.concatenate([turned[0:4] + turned[4:8] + turned[8:12], jnp.zeros((4, GROUP), F32)], axis=0)
        return carry

    lax.fori_loop(0, length // GROUP, reorder, 0)

    some = pl.ds(0, chips - 1)
    pltpu.make_async_copy(rs_recv.at[some], rs_recv.at[some], rs_sem.at[1]).wait()
    total = jnp.zeros((8, 512), F32)
    total_cos = jnp.zeros((8, 512), F32)
    total_sin = jnp.zeros((8, 512), F32)
    for zz in range(chips):
        part = rs_recv[zz].astype(F32)
        total = total + part
        total_cos = total_cos + phase_v[zz, 0:1, 0:1] * part
        total_sin = total_sin + phase_v[zz, 1:2, 0:1] * part
    masks = pick_v[0]
    blocks = [total * masks[r : r + 1] for r in range(6)]
    blocks.append(total_cos * masks[0:1] + total_sin * masks[1:2])
    blocks.append(total_cos * masks[1:2] - total_sin * masks[0:1])
    block_rows = dot(jnp.concatenate(blocks, axis=0), fold_v[0], PRECISE)
    tails = [pltpu.roll(t[:, 384:512], LANES - 48, 1) for t in (total, total_cos, total_sin)]
    weighted = jnp.concatenate(
        [tails[0][0:6], tails[1][0:1] + tails[2][1:2], tails[1][1:2] - tails[2][0:1]], axis=0
    )
    first = dot(block_rows, terms[0], PRECISE)
    second = dot(weighted, terms[1], PRECISE)
    products = []
    for p in range(NMOM):
        first_re, first_im = first[16 * p : 16 * p + 8], first[16 * p + 8 : 16 * p + 16]
        second_re, second_im = second[2 * p : 2 * p + 1], second[2 * p + 1 : 2 * p + 2]
        products.append(first_re * second_re - first_im * second_im)
        products.append(first_re * second_im + first_im * second_re)
    coeffs = dot_nt(jnp.concatenate(products, axis=0), terms[2], PRECISE)
    piece = jnp.concatenate([coeffs[8 * b : 8 * b + 8, 0:72] for b in range(8)] + [jnp.zeros((8, 64), F32)], axis=1)
    member, quad = lax.rem(z, 4), z // 4
    quads = chips // 4
    gathered[core, member, quad] = piece.astype(BF16)

    def send_far(i, carry):
        peer = lax.rem(quad + far_first(i, quads), quads)
        mine = gathered.at[core, member, quad]
        remote(mine, mine, near_sem.at[0], ag_sem.at[quad], 4 * peer + member, core).start()
        return carry

    lax.fori_loop(0, quads - 1, send_far, 0)

    def spread(came):
        for o in (2, 1, 3):
            remote(came, came, near_sem.at[1], side_sem.at[member], 4 * quad + lax.rem(member + o, 4), core).start()

    spread(gathered.at[core, member, quad])

    def hand_on(i, carry):
        peer = lax.rem(quad + far_first(quads - 2 - i, quads), quads)
        came = gathered.at[core, member, peer]
        pltpu.make_async_copy(came, came, ag_sem.at[peer]).wait()
        spread(came)
        return carry

    lax.fori_loop(0, quads - 1, hand_on, 0)
    for o in range(4):
        whose = lax.rem(member + o, 4)
        theirs = gathered.at[core, whose]
        if o:
            pltpu.make_async_copy(theirs, theirs, side_sem.at[whose]).wait()
        remote(theirs, theirs, both_send, both_sem.at[whose], z, other).start()
    for o in range(4):
        theirs = gathered.at[other, o]
        pltpu.make_async_copy(theirs, theirs, both_sem.at[o]).wait()

    for h in range(2):
        for lb in range(5):
            lanes = slice(lb * LANES, (lb + 1) * LANES)
            tall = jnp.concatenate([gathered[h, zz % 4, zz // 4, :, lanes].astype(F32) for zz in range(chips)], axis=0)
            coeff_t[h, lanes] = tall.T
    for a in range(3):
        def rows_of(q, sign=1.0):
            taken = [
                coeff_t[h, (2 * p + q) * 72 + a * HALF : (2 * p + q) * 72 + (a + 1) * HALF]
                for p in range(NMOM)
                for h in range(2)
            ]
            return (sign * jnp.concatenate(taken, axis=0)).astype(BF16)

        left[a, 0:192, 0:NVEC] = rows_of(0)
        left[a, 0:192, NVEC:] = rows_of(1, -1.0)
        left[a, 192:384, 0:NVEC] = rows_of(1)
        left[a, 192:384, NVEC:] = rows_of(0)

    cos_z, sin_z = phase_v[z, 0:1, 0:1], phase_v[z, 1:2, 0:1]
    groups = length // GROUP
    my_group = me // 8

    def rebuild(i, carry):
        g = lax.rem(my_group + jnp.where(i == groups - 1, 0, far_first(i, groups)), groups)
        columns = pl.ds(pl.multiple_of(g * GROUP, GROUP), GROUP)
        table = phase_p[:, columns]
        cos_x, sin_x, cos_y, sin_y = (table[n : n + 1] for n in range(4))
        for a in range(3):
            both = dot(left[a], eig_p[a, :, columns])
            re = [both[48 * p : 48 * p + 48] for p in range(NMOM)]
            im = [both[192 + 48 * p : 240 + 48 * p] for p in range(NMOM)]
            out_re = re[0] + (cos_x * re[1] - sin_x * im[1]) + (cos_y * re[2] - sin_y * im[2]) + (cos_z * re[3] - sin_z * im[3])
            out_im = im[0] + (cos_x * im[1] + sin_x * re[1]) + (cos_y * im[2] + sin_y * re[2]) + (cos_z * im[3] + sin_z * re[3])
            source[48 * a : 48 * a + 48] = out_re * scale_out
            source[144 + 48 * a : 192 + 48 * a] = out_im * scale_out
        for k in range(2):
            tiles = [source[72 * q : 72 * q + 72, k * LANES : (k + 1) * LANES] for q in range(4)]
            for n, message in enumerate(swap_blocks(tiles, lane_blocks())):
                to_send[g * 8 + 4 * k + n] = message.reshape(9, 8, LANES).astype(BF16)
        for n in range(8):
            peer = g * 8 + n

            @pl.when(peer != me)
            def _():
                remote(to_send.at[peer], arrived.at[me], all_send, all_sem.at[z // 2], peer // 2, n % 2).start()

        return carry

    lax.fori_loop(0, groups, rebuild, 0)
    arrived[me] = to_send[me]

    source_pairs = chips // 2

    def place(group):
        tiles = [arrived[4 * group + d].astype(F32).reshape(72, LANES) for d in range(4)]
        rows = jnp.concatenate(swap_blocks(tiles, lane_blocks()), axis=0)
        columns = pl.ds(pl.multiple_of(group * LANES, LANES), LANES)
        for q in range(2):
            for a in range(3):
                base = q * 144 + a * 48
                result[q, a, :, :, columns] = rows[base : base + 48].reshape(12, 4, LANES).astype(BF16)
        pltpu.make_async_copy(result.at[:, :, :, :, columns], out.at[:, :, :, :, columns], out_sem).start()

    def finish(i, carry):
        group = lax.rem(z // 2 + far_first(i, source_pairs), source_pairs)
        four = arrived.at[pl.ds(4 * group, 4)]
        pltpu.make_async_copy(four, four, all_sem.at[group]).wait()
        place(group)
        return carry

    lax.fori_loop(0, source_pairs - 1, finish, 0)
    three = arrived.at[pl.ds(0, 3)]
    pltpu.make_async_copy(three, three, all_sem.at[z // 2]).wait()
    place(z // 2)

    def drain(ref, sem):
        pltpu.make_async_copy(ref, ref, sem).wait()

    drain(idx_recv.at[pl.ds(0, devices - 1)], idx_sem.at[0])
    drain(rs_send.at[pl.ds(0, chips - 1)], rs_sem.at[0])
    drain(gathered.at[0, 0, pl.ds(0, quads - 1)], near_sem.at[0])
    drain(gathered.at[0, pl.ds(0, 3)], near_sem.at[1])
    drain(gathered.at[0], both_send)
    drain(to_send.at[pl.ds(0, devices - 1)], all_send)
    drain(result, out_sem)


def on_device(propagator, eigvecs, operator_weights, sink_time, term_index, term_sign, solver_order):
    length = propagator.shape[-1]
    chips = lax.axis_size("space_0")
    devices = lax.axis_size(SPACE)
    scale_in = 1.0 / math.sqrt(3.0 * length * devices)
    scale_out = 1.0 / math.sqrt(NMOM * NVEC)
    tables, pieces, chip_phase, pick, fold = fixed_tables(length, chips)
    hbm = pl.BlockSpec(memory_space=pl.ANY)
    arrived = pltpu.VMEM((devices, 9, 8, LANES), BF16)
    result = pl.pallas_call(
        functools.partial(whole_kernel, chips, length, scale_in, scale_out),
        out_shape=jax.ShapeDtypeStruct((2, 3, 12, 4, length), BF16),
        in_specs=[hbm] * 12,
        out_specs=hbm,
        scratch_shapes=[
            pltpu.VMEM((3, 2 * NVEC, length), BF16),
            pltpu.VMEM((2, 3, 12, 4, length), BF16),
            pltpu.VMEM(operator_weights.shape, F32),
            pltpu.VMEM((1, 1), jnp.int32),
            pltpu.VMEM((devices // 4, LANES), jnp.int32),
            pltpu.VMEM((3, NTERM), jnp.int32),
            pltpu.VMEM((1, NTERM), jnp.int32),
            pltpu.VMEM(tables.shape[1:], F32),
            pltpu.VMEM(pieces.shape[1:], BF16),
            pltpu.VMEM(chip_phase.shape, F32),
            pltpu.VMEM(pick.shape, F32),
            pltpu.VMEM(fold.shape, F32),
            pltpu.VMEM((2, 3, NVEC, 144), F32),
            pltpu.VMEM((2, NVEC, 512), F32),
            pltpu.VMEM((NVEC, 512), F32),
            pltpu.VMEM((NVEC, 512), F32),
            pltpu.VMEM((chips, 8, 512), BF16),
            pltpu.VMEM((chips, 8, 512), BF16),
            pltpu.VMEM((4, devices // 4, 1, LANES), jnp.int32),
            pltpu.VMEM((devices, 1, LANES), jnp.int32),
            pltpu.VMEM((3, LANES, 384), F32),
            pltpu.VMEM((length, GROUP), BF16),
            pltpu.VMEM((3, 2 * NVEC, length), BF16),
            pltpu.VMEM((8, length), F32),
            pltpu.VMEM((2, 4, chips // 4, 8, 640), BF16),
            pltpu.VMEM((2, 640, NVEC), F32),
            pltpu.VMEM((3, 384, 2 * NVEC), BF16),
            pltpu.VMEM((288, GROUP), F32),
            arrived,
            arrived,
            pltpu.VMEM((2, 3, 12, 4, length), BF16),
            pltpu.SemaphoreType.DMA((12,)),
            pltpu.SemaphoreType.DMA((10,)),
            pltpu.SemaphoreType.DMA((2,)),
            pltpu.SemaphoreType.DMA((2,)),
            pltpu.SemaphoreType.DMA((2,)),
            pltpu.SemaphoreType.DMA((2,)),
            pltpu.SemaphoreType.DMA((chips // 4,)),
            pltpu.SemaphoreType.DMA((4,)),
            pltpu.SemaphoreType.DMA,
            pltpu.SemaphoreType.DMA((4,)),
            pltpu.SemaphoreType.DMA,
            pltpu.SemaphoreType.DMA((chips // 2,)),
            pltpu.SemaphoreType.DMA,
        ],
        compiler_params=pltpu.CompilerParams(collective_id=0, has_side_effects=True, vmem_limit_bytes=56 * 2**20),
    )(
        eigvecs, jnp.swapaxes(propagator, 2, 3), operator_weights, sink_time.reshape(1, 1), solver_order.reshape(devices // 4, LANES),
        term_index.T, term_sign.reshape(1, -1), jnp.asarray(tables), jnp.asarray(pieces), jnp.asarray(chip_phase),
        jnp.asarray(pick), jnp.asarray(fold),
    )
    return jnp.swapaxes(result, 2, 3)


def solution(mesh):
    finer = Mesh(mesh.devices.reshape(mesh.shape["grp"], -1, 2), ("grp", "space_0", "space_1"))
    in_specs = (
        P("grp", None, None, None, SPACE),
        P("grp", None, None, SPACE),
        P("grp", None, None),
        P("grp"),
        P(),
        P(),
        P(SPACE),
    )
    out_specs = P("grp", None, None, None, SPACE)
    return jax.shard_map(on_device, mesh=finer, in_specs=in_specs, out_specs=out_specs, check_vma=False)
```

time: 208 us -> 190 us (0.913)
  Pallas kernels: 196 us -> 187 us
  local copies, waits for them, and re-layouts: 7.84 us -> 2.93 us
  other arithmetic: 2.39 us -> 0 us
    pallas_call x1, Pallas kernels: 192 us -> 187 us  [on_device(): pl.pallas_call(functools.partial(whole_kernel, chips, length, scale_in, s...]
    pallas_call x1 -> x0, Pallas kernels: 4.15 us -> none  [on_device(): pl.pallas_call(format_kernel, out_shape=jax.ShapeDtypeStruct((2, 3, 4, 12...]
    pallas_call x1 -> x0, local copies, waits for them, and re-layouts: 3.34 us -> none  [on_device(): pl.pallas_call(format_kernel, out_shape=jax.ShapeDtypeStruct((2, 3, 4, 12...]
where the time goes in v2:
time: 190 us
  Pallas kernels  187 us (98%)
  local copies, waits for them, and re-layouts  2.93 us (2%)
    pallas_call x1, Pallas kernels, on_device(): pl.pallas_call(functools.partial(whole_kernel, chips, length, scale_in, s...  187 us

profile of v2, /device:TPU:37, one launch (start us, length us, event | category | flops | bytes accessed | tf_op | source)
XLA Modules:
  0.0 190.3 jit_solution(13940317684365754061)
XLA Ops:
  0.7 186.7 %shard_map.118 = bf16[2,3,12,4,2048]{4,3,2,1,0:T(4,128)(2,1)} custom-call(bf16[2,3,256,2048]{3,2,1,0:T(8,128)(2,1)} %eig.1, bf16[2,3,12,4,2048]{4,3,2,1,0:T(4,128)(2,1)} %bitcast.8, f32[128,2,256]{2,1,0:T(2,128)} %op_weights.1, s32[1,1]{1,0:T(1,128)} %bitcast.6.sink, s32[16,128]{1,0:T(8,128)} %bitcast.9, s32[3,48]{1,0:T(4,128)} %bitcast.10, ...), custom_call_target="tpu_custom_call" | custom-call | tf_op jit(solution)/shard_map/pallas_call | solution.py:437
  187.4 2.9 %copy.15 = bf16[2,3,4,12,2048]{4,2,3,1,0:T(4,128)(2,1)} copy(bf16[2,3,4,12,2048]{4,2,3,1,0:T(4,128)(2,1)} %bitcast.7) | data formatting | bytes 2359296

commit v3 on v2

--- a/solution.py
+++ b/solution.py
@@ -196,14 +196,8 @@
     for load in late_loads:
         load.wait()
 
-    lane_block = lax.broadcasted_iota(jnp.int32, (devices // 4, LANES), 1) // 32
-    my_block = lax.rem(me, 4)
     for k in range(4):
-        moved = jnp.zeros((devices // 4, LANES), jnp.int32)
-        for t in range(4):
-            turned = order_v[...] if t == k else pltpu.roll(order_v[...], ((t - k) * 32) % LANES, 1)
-            moved = jnp.where((lane_block == t) & (my_block == t), turned, moved)
-        idx_send[k] = moved.reshape(devices // 4, 1, LANES)
+        idx_send[k] = order_v[:, 32 * k : 32 * k + 32].reshape(devices // 4, 1, 32)
     for n, matrix in enumerate(term_matrices(index_v[...], sign_v[...])):
         terms[n] = matrix
     pl.semaphore_wait(barrier, devices - 1)
@@ -220,7 +214,7 @@
 
     lax.fori_loop(0, chips - 1, send_index, 0)
     remote(idx_send.at[2 * lax.rem(z, 2) + other, z // 2], idx_recv.at[me], idx_sem.at[0], idx_sem.at[1], z, other).start()
-    idx_recv[me] = idx_send[my_block, z // 2]
+    idx_recv[me] = idx_send[lax.rem(me, 4), z // 2]
 
     to_core.wait()
     chip_sum[...] = (full[core] + from_core[...]) * scale_in
@@ -253,9 +247,7 @@
 
     def reorder(g, carry):
         columns = pl.ds(pl.multiple_of(g * GROUP, GROUP), GROUP)
-        wanted = jnp.concatenate(
-            [sum(idx_recv[g * 8 + 4 * k + n] for n in range(4)) for k in range(2)], axis=1
-        ) - me * length
+        wanted = jnp.concatenate([idx_recv[g * 8 + n] for n in range(8)], axis=1) - me * length
 
         def one_hot(rb, inner):
             rows = pl.ds(pl.multiple_of(rb * 64, 64), 64)
@@ -458,8 +450,8 @@
             pltpu.VMEM((NVEC, 512), F32),
             pltpu.VMEM((chips, 8, 512), BF16),
             pltpu.VMEM((chips, 8, 512), BF16),
-            pltpu.VMEM((4, devices // 4, 1, LANES), jnp.int32),
-            pltpu.VMEM((devices, 1, LANES), jnp.int32),
+            pltpu.VMEM((4, devices // 4, 1, 32), jnp.int32),
+            pltpu.VMEM((devices, 1, 32), jnp.int32),
             pltpu.VMEM((3, LANES, 384), F32),
             pltpu.VMEM((length, GROUP), BF16),
             pltpu.VMEM((3, 2 * NVEC, length), BF16),

time: 190 us -> 190 us (level)
  no operation moved by 1% of the time
where the time goes in v3:
time: 190 us
  Pallas kernels  186 us (98%)
  local copies, waits for them, and re-layouts  2.93 us (2%)
    pallas_call x1, Pallas kernels, on_device(): pl.pallas_call(functools.partial(whole_kernel, chips, length, scale_in, s...  186 us

profile of v3, /device:TPU:37, one launch (start us, length us, event | category | flops | bytes accessed | tf_op | source)
XLA Modules:
  0.0 190.0 jit_solution(13361175977320075267)
XLA Ops:
  0.7 186.4 %shard_map.118 = bf16[2,3,12,4,2048]{4,3,2,1,0:T(4,128)(2,1)} custom-call(bf16[2,3,256,2048]{3,2,1,0:T(8,128)(2,1)} %eig.1, bf16[2,3,12,4,2048]{4,3,2,1,0:T(4,128)(2,1)} %bitcast.8, f32[128,2,256]{2,1,0:T(2,128)} %op_weights.1, s32[1,1]{1,0:T(1,128)} %bitcast.6.sink, s32[16,128]{1,0:T(8,128)} %bitcast.9, s32[3,48]{1,0:T(4,128)} %bitcast.10, ...), custom_call_target="tpu_custom_call" | custom-call | tf_op jit(solution)/shard_map/pallas_call | solution.py:429
  187.1 2.9 %copy.15 = bf16[2,3,4,12,2048]{4,2,3,1,0:T(4,128)(2,1)} copy(bf16[2,3,4,12,2048]{4,2,3,1,0:T(4,128)(2,1)} %bitcast.7) | data formatting | bytes 2359296
